TPU v7x, 256 devices: a whole 4x4x8 slice. The times are simulated.
256 devices in a mesh: gx: 4 (over x), gy: 4 (over z_hi), gz: 16 (over z_lo, y, core).
Axes of the slice: x: 4, y: 4, z: 8 (z_hi: 4, z_lo: 2; z = z_hi * 2 + z_lo), core: 2. Of those that a mesh axis runs over, the one named last changes fastest.
Arguments:
- columns: int32 [8192, 2048], P(('gx', 'gy', 'gz')), may hold values from 0 to 32767, as said below
- counts: int32 [8192, 2048], P(('gx', 'gy', 'gz')), may hold values from 1 to 63
- nnz_count: int32 [8192], P(('gx', 'gy', 'gz')), may hold values from 1 to 2048, as said below
- selected: int32 [2048], replicated, may hold values from 0 to 32767, as said below
Outputs:
- gene_stats: float32 [2, 32768], P(None, 'gz')
- pca_input: bfloat16 [8192, 2048], P(('gx', 'gy'), 'gz')
Inputs may be any that keep to these rules, and one draw needn't show every extreme that they name: `columns`: in each row no two slots fall in the same block of 16 consecutive genes (so the first nnz_count slots hold distinct genes); slots beyond nnz_count are not part of the matrix. For every k, the live slots of one cell fall on at most 16 of the genes selected[k * 2048 / 16] to selected[(k + 1) * 2048 / 16 - 1]; some cell reaches 16 for every k in every draw. `nnz_count`: some cell has all 2048 slots live in every draw. `selected`: distinct genes.
All inputs are finite; a program needn't handle non-finite values.
Results may differ from a plain program's by a relative error of at most 0.0085.
Values may be sent and summed in bfloat16 or wider, within the bound.
A program may use at most 128 MiB of HBM per device.

v0:
```python
import jax
import jax.numpy as jnp
from jax import lax
from jax.sharding import PartitionSpec as P

GENES = 32768
SEL = 2048


target_sum = 10000.0
var_floor = 0.01
clip_value = 10.0
lane_count = 256


def split_up(value, dim, length):
    dims = value.shape
    tiles = value.reshape(*dims[:dim], length, dims[dim] // length, *dims[dim + 1 :])
    return jnp.moveaxis(tiles, dim, 0)


def sum_at_owner(value, axis, dim):
    length = lax.axis_size(axis)
    tiles = lax.all_to_all(split_up(value, dim, length), axis, 0, 0, tiled=True)
    return jnp.sum(tiles.astype(jnp.float32), axis=0)


def copy_for_each(value, axis):
    copies = jnp.broadcast_to(value, (lax.axis_size(axis), *value.shape))
    return lax.all_to_all(copies, axis, split_axis=0, concat_axis=0, tiled=True)


def of_everyone(value, axis):
    everything = copy_for_each(value, axis)
    return jnp.sum(everything, axis=0)


def standardize(dense, mean_sel, variance_sel):
    scale_sel = jnp.sqrt(jnp.maximum(variance_sel, var_floor))
    return jnp.clip((dense - mean_sel[None, :]) / scale_sel[None, :], -clip_value, clip_value)


def cell_block(pair):
    block_genes, block_values = pair
    high_count = GENES // lane_count
    high_ids = lax.broadcasted_iota(jnp.int32, (1, 1, high_count), 2)
    low_ids = lax.broadcasted_iota(jnp.int32, (1, 1, lane_count), 2)
    high_table = ((block_genes // lane_count)[:, :, None] == high_ids).astype(jnp.bfloat16)
    low_hit = (block_genes % lane_count)[:, :, None] == low_ids
    upper = lax.optimization_barrier(block_values.astype(jnp.bfloat16))
    lower = (block_values - upper.astype(jnp.float32)).astype(jnp.bfloat16)
    upper_table = jnp.where(low_hit, upper[:, :, None], jnp.bfloat16(0.0))
    lower_table = jnp.where(low_hit, lower[:, :, None], jnp.bfloat16(0.0))
    upper_part = jnp.einsum(
        "csh,csl->chl", high_table, upper_table, preferred_element_type=jnp.float32
    )
    lower_part = jnp.einsum(
        "csh,csl->chl", high_table, lower_table, preferred_element_type=jnp.float32
    )
    return upper_part + lower_part


def per_device(columns, counts, nnz_count, selected):
    local_cells = columns.shape[0]
    row_slots = columns.shape[1]
    owners = lax.axis_size("gz")
    owner_index = lax.axis_index("gz")
    cells = local_cells * lax.axis_size("gx") * lax.axis_size("gy") * owners
    slot = lax.broadcasted_iota(jnp.int32, counts.shape, 1)
    live = slot < nnz_count[:, None]
    raw = jnp.where(live, counts.astype(jnp.float32), jnp.float32(0.0))
    library = jnp.sum(raw, axis=1, keepdims=True)
    values = jnp.log1p(raw * (target_sum / library))
    genes = jnp.where(live, columns, 0)
    block_rows = 4
    block_total = local_cells // block_rows
    expanded = lax.map(
        cell_block,
        (
            genes.reshape(block_total, block_rows, row_slots),
            values.reshape(block_total, block_rows, row_slots),
        ),
    )
    expanded = expanded.reshape(local_cells, GENES)
    total = jnp.sum(expanded, axis=0)
    square = jnp.sum(expanded * expanded, axis=0)
    terms = jnp.stack([total, square])
    owned = GENES // owners
    shares = sum_at_owner(terms.astype(jnp.bfloat16), "gz", 1)
    own_sums = of_everyone(shares, ("gx", "gy"))
    local_index = selected - owner_index * owned
    inside = (local_index >= 0) & (local_index < owned)
    fetched = jnp.take(own_sums, jnp.clip(local_index, 0, owned - 1), axis=1)
    partial_picked = jnp.where(inside[None, :], fetched, jnp.float32(0.0))
    picked_sums = of_everyone(partial_picked, "gz")
    own_mean = own_sums[0] / cells
    own_variance = own_sums[1] / cells - own_mean * own_mean
    gene_stats = jnp.stack([own_mean, own_variance])
    sel_mean = picked_sums[0] / cells
    sel_variance = picked_sums[1] / cells - sel_mean * sel_mean
    dense = jnp.take(expanded, selected, axis=1)
    share_size = SEL // owners
    own_mean_sel = lax.dynamic_slice_in_dim(sel_mean, owner_index * share_size, share_size, 0)
    own_variance_sel = lax.dynamic_slice_in_dim(
        sel_variance, owner_index * share_size, share_size, 0
    )
    moved = lax.all_to_all(
        dense.astype(jnp.bfloat16), "gz", split_axis=1, concat_axis=0, tiled=True
    ).astype(dense.dtype)
    pca_input = standardize(moved, own_mean_sel, own_variance_sel).astype(jnp.bfloat16)
    return (gene_stats, pca_input)


def solution(mesh):
    return jax.shard_map(
        per_device,
        mesh=mesh,
        in_specs=(
            P(("gx", "gy", "gz"), None),
            P(("gx", "gy", "gz"), None),
            P(("gx", "gy", "gz")),
            P(),
        ),
        out_specs=(P(None, "gz"), P(("gx", "gy"), "gz")),
        check_vma=False,
    )
```

profile of v0, /device:TPU:1, one launch (start us, length us, event | category | flops | bytes accessed | tf_op | source)
XLA Modules:
  0.0 140.7 jit_solution(2179630809846439621)
XLA Ops:
  0.6 1.2 fusion.32
  1.8 1.1 multiply_log-plus-one_fusion
  3.0 0.1 reshape.116
  3.0 1.0 fusion.31
  4.1 0.1 reshape.115
  4.2 56.9 %while.12 = (s32[]{:T(128)}, f32[8,4,128,256]{3,2,1,0:T(8,128)}, s32[8,4,2048]{2,1,0:T(4,128)S(1)}, f32[8,4,2048]{2,1,0:T(4,128)S(1)}, s32[]{:T(128)}) while((s32[]{:T(128)}, f32[8,4,128,256]{3,2,1,0:T(8,128)}, s32[8,4,2048]{2,1,0:T(4,128)S(1)}, f32[8,4,2048]{2,1,0:T(4,128)S(1)}, s32[]{:T(128)}) %tuple.42), condition=%wide.region_2.3_spmd, body=%wide.region_1.2_spmd.sunk | while | flops 1084588032 | bytes 1982553 | solution.py:77
  4.2 0.1 add_select_fusion.4
  4.3 3.2 %fusion.46 = f32[4,128,256]{2,1,0:T(8,128)S(1)} fusion(s32[4,2048]{1,0:T(4,128)S(1)} %add_select_fusion.5, bf16[4,2048]{1,0:T(4,128)(2,1)S(1)} %bitcast_convert_fusion.2, s32[4,2048]{1,0:T(4,128)S(1)} %get-tuple-element.114), kind=kOutput, calls=%fused_computation.5.clone.1 | convolution fusion | flops 542113792 | bytes 606208 | tf_op jit(solution)/shard_map/while/body/eval_jaxpr/csh,csl->chl/dot_general | solution.py:54
  7.5 3.8 %fusion.48 = f32[8,4,128,256]{3,2,1,0:T(8,128)} fusion(f32[8,4,128,256]{3,2,1,0:T(8,128)} %get-tuple-element.121, s32[]{:T(128)S(6)} %copy.49, f32[4,128,256]{2,1,0:T(8,128)S(1)} %fusion.46, s32[4,2048]{1,0:T(4,128)S(1)} %add_select_fusion.5, bf16[4,2048]{1,0:T(4,128)(2,1)S(1)} %fusion.47, s32[4,2048]{1,0:T(4,128)S(1)} %get-tuple-element.114), kind=kOutput, calls=%fused_computation.18.clone.1 | convolution fusion | flops 542244864 | bytes 1130500 | tf_op jit(solution)/shard_map/while/body/eval_jaxpr/csh,csl->chl/dot_general | solution.py:57
  11.4 3.2 %fusion.46 = f32[4,128,256]{2,1,0:T(8,128)S(1)} fusion(s32[4,2048]{1,0:T(4,128)S(1)} %add_select_fusion.5, bf16[4,2048]{1,0:T(4,128)(2,1)S(1)} %bitcast_convert_fusion.2, s32[4,2048]{1,0:T(4,128)S(1)} %get-tuple-element.114), kind=kOutput, calls=%fused_computation.5.clone.1 | convolution fusion | flops 542113792 | bytes 606208 | tf_op jit(solution)/shard_map/while/body/eval_jaxpr/csh,csl->chl/dot_general | solution.py:54
  14.6 3.8 %fusion.48 = f32[8,4,128,256]{3,2,1,0:T(8,128)} fusion(f32[8,4,128,256]{3,2,1,0:T(8,128)} %get-tuple-element.121, s32[]{:T(128)S(6)} %copy.49, f32[4,128,256]{2,1,0:T(8,128)S(1)} %fusion.46, s32[4,2048]{1,0:T(4,128)S(1)} %add_select_fusion.5, bf16[4,2048]{1,0:T(4,128)(2,1)S(1)} %fusion.47, s32[4,2048]{1,0:T(4,128)S(1)} %get-tuple-element.114), kind=kOutput, calls=%fused_computation.18.clone.1 | convolution fusion | flops 542244864 | bytes 1130500 | tf_op jit(solution)/shard_map/while/body/eval_jaxpr/csh,csl->chl/dot_general | solution.py:57
  18.6 3.2 %fusion.46 = f32[4,128,256]{2,1,0:T(8,128)S(1)} fusion(s32[4,2048]{1,0:T(4,128)S(1)} %add_select_fusion.5, bf16[4,2048]{1,0:T(4,128)(2,1)S(1)} %bitcast_convert_fusion.2, s32[4,2048]{1,0:T(4,128)S(1)} %get-tuple-element.114), kind=kOutput, calls=%fused_computation.5.clone.1 | convolution fusion | flops 542113792 | bytes 606208 | tf_op jit(solution)/shard_map/while/body/eval_jaxpr/csh,csl->chl/dot_general | solution.py:54
  21.7 3.8 %fusion.48 = f32[8,4,128,256]{3,2,1,0:T(8,128)} fusion(f32[8,4,128,256]{3,2,1,0:T(8,128)} %get-tuple-element.121, s32[]{:T(128)S(6)} %copy.49, f32[4,128,256]{2,1,0:T(8,128)S(1)} %fusion.46, s32[4,2048]{1,0:T(4,128)S(1)} %add_select_fusion.5, bf16[4,2048]{1,0:T(4,128)(2,1)S(1)} %fusion.47, s32[4,2048]{1,0:T(4,128)S(1)} %get-tuple-element.114), kind=kOutput, calls=%fused_computation.18.clone.1 | convolution fusion | flops 542244864 | bytes 1130500 | tf_op jit(solution)/shard_map/while/body/eval_jaxpr/csh,csl->chl/dot_general | solution.py:57
  25.7 3.2 %fusion.46 = f32[4,128,256]{2,1,0:T(8,128)S(1)} fusion(s32[4,2048]{1,0:T(4,128)S(1)} %add_select_fusion.5, bf16[4,2048]{1,0:T(4,128)(2,1)S(1)} %bitcast_convert_fusion.2, s32[4,2048]{1,0:T(4,128)S(1)} %get-tuple-element.114), kind=kOutput, calls=%fused_computation.5.clone.1 | convolution fusion | flops 542113792 | bytes 606208 | tf_op jit(solution)/shard_map/while/body/eval_jaxpr/csh,csl->chl/dot_general | solution.py:54
  28.8 3.8 %fusion.48 = f32[8,4,128,256]{3,2,1,0:T(8,128)} fusion(f32[8,4,128,256]{3,2,1,0:T(8,128)} %get-tuple-element.121, s32[]{:T(128)S(6)} %copy.49, f32[4,128,256]{2,1,0:T(8,128)S(1)} %fusion.46, s32[4,2048]{1,0:T(4,128)S(1)} %add_select_fusion.5, bf16[4,2048]{1,0:T(4,128)(2,1)S(1)} %fusion.47, s32[4,2048]{1,0:T(4,128)S(1)} %get-tuple-element.114), kind=kOutput, calls=%fused_computation.18.clone.1 | convolution fusion | flops 542244864 | bytes 1130500 | tf_op jit(solution)/shard_map/while/body/eval_jaxpr/csh,csl->chl/dot_general | solution.py:57
  32.8 3.2 %fusion.46 = f32[4,128,256]{2,1,0:T(8,128)S(1)} fusion(s32[4,2048]{1,0:T(4,128)S(1)} %add_select_fusion.5, bf16[4,2048]{1,0:T(4,128)(2,1)S(1)} %bitcast_convert_fusion.2, s32[4,2048]{1,0:T(4,128)S(1)} %get-tuple-element.114), kind=kOutput, calls=%fused_computation.5.clone.1 | convolution fusion | flops 542113792 | bytes 606208 | tf_op jit(solution)/shard_map/while/body/eval_jaxpr/csh,csl->chl/dot_general | solution.py:54
  35.9 3.8 %fusion.48 = f32[8,4,128,256]{3,2,1,0:T(8,128)} fusion(f32[8,4,128,256]{3,2,1,0:T(8,128)} %get-tuple-element.121, s32[]{:T(128)S(6)} %copy.49, f32[4,128,256]{2,1,0:T(8,128)S(1)} %fusion.46, s32[4,2048]{1,0:T(4,128)S(1)} %add_select_fusion.5, bf16[4,2048]{1,0:T(4,128)(2,1)S(1)} %fusion.47, s32[4,2048]{1,0:T(4,128)S(1)} %get-tuple-element.114), kind=kOutput, calls=%fused_computation.18.clone.1 | convolution fusion | flops 542244864 | bytes 1130500 | tf_op jit(solution)/shard_map/while/body/eval_jaxpr/csh,csl->chl/dot_general | solution.py:57
  39.9 3.2 %fusion.46 = f32[4,128,256]{2,1,0:T(8,128)S(1)} fusion(s32[4,2048]{1,0:T(4,128)S(1)} %add_select_fusion.5, bf16[4,2048]{1,0:T(4,128)(2,1)S(1)} %bitcast_convert_fusion.2, s32[4,2048]{1,0:T(4,128)S(1)} %get-tuple-element.114), kind=kOutput, calls=%fused_computation.5.clone.1 | convolution fusion | flops 542113792 | bytes 606208 | tf_op jit(solution)/shard_map/while/body/eval_jaxpr/csh,csl->chl/dot_general | solution.py:54
  43.0 3.8 %fusion.48 = f32[8,4,128,256]{3,2,1,0:T(8,128)} fusion(f32[8,4,128,256]{3,2,1,0:T(8,128)} %get-tuple-element.121, s32[]{:T(128)S(6)} %copy.49, f32[4,128,256]{2,1,0:T(8,128)S(1)} %fusion.46, s32[4,2048]{1,0:T(4,128)S(1)} %add_select_fusion.5, bf16[4,2048]{1,0:T(4,128)(2,1)S(1)} %fusion.47, s32[4,2048]{1,0:T(4,128)S(1)} %get-tuple-element.114), kind=kOutput, calls=%fused_computation.18.clone.1 | convolution fusion | flops 542244864 | bytes 1130500 | tf_op jit(solution)/shard_map/while/body/eval_jaxpr/csh,csl->chl/dot_general | solution.py:57
  47.0 3.2 %fusion.46 = f32[4,128,256]{2,1,0:T(8,128)S(1)} fusion(s32[4,2048]{1,0:T(4,128)S(1)} %add_select_fusion.5, bf16[4,2048]{1,0:T(4,128)(2,1)S(1)} %bitcast_convert_fusion.2, s32[4,2048]{1,0:T(4,128)S(1)} %get-tuple-element.114), kind=kOutput, calls=%fused_computation.5.clone.1 | convolution fusion | flops 542113792 | bytes 606208 | tf_op jit(solution)/shard_map/while/body/eval_jaxpr/csh,csl->chl/dot_general | solution.py:54
  50.2 3.8 %fusion.48 = f32[8,4,128,256]{3,2,1,0:T(8,128)} fusion(f32[8,4,128,256]{3,2,1,0:T(8,128)} %get-tuple-element.121, s32[]{:T(128)S(6)} %copy.49, f32[4,128,256]{2,1,0:T(8,128)S(1)} %fusion.46, s32[4,2048]{1,0:T(4,128)S(1)} %add_select_fusion.5, bf16[4,2048]{1,0:T(4,128)(2,1)S(1)} %fusion.47, s32[4,2048]{1,0:T(4,128)S(1)} %get-tuple-element.114), kind=kOutput, calls=%fused_computation.18.clone.1 | convolution fusion | flops 542244864 | bytes 1130500 | tf_op jit(solution)/shard_map/while/body/eval_jaxpr/csh,csl->chl/dot_general | solution.py:57
  54.1 3.2 %fusion.46 = f32[4,128,256]{2,1,0:T(8,128)S(1)} fusion(s32[4,2048]{1,0:T(4,128)S(1)} %add_select_fusion.5, bf16[4,2048]{1,0:T(4,128)(2,1)S(1)} %bitcast_convert_fusion.2, s32[4,2048]{1,0:T(4,128)S(1)} %get-tuple-element.114), kind=kOutput, calls=%fused_computation.5.clone.1 | convolution fusion | flops 542113792 | bytes 606208 | tf_op jit(solution)/shard_map/while/body/eval_jaxpr/csh,csl->chl/dot_general | solution.py:54
  57.3 3.8 %fusion.48 = f32[8,4,128,256]{3,2,1,0:T(8,128)} fusion(f32[8,4,128,256]{3,2,1,0:T(8,128)} %get-tuple-element.121, s32[]{:T(128)S(6)} %copy.49, f32[4,128,256]{2,1,0:T(8,128)S(1)} %fusion.46, s32[4,2048]{1,0:T(4,128)S(1)} %add_select_fusion.5, bf16[4,2048]{1,0:T(4,128)(2,1)S(1)} %fusion.47, s32[4,2048]{1,0:T(4,128)S(1)} %get-tuple-element.114), kind=kOutput, calls=%fused_computation.18.clone.1 | convolution fusion | flops 542244864 | bytes 1130500 | tf_op jit(solution)/shard_map/while/body/eval_jaxpr/csh,csl->chl/dot_general | solution.py:57
  61.1 2.6 %fusion.38 = (bf16[128,256]{1,0:T(8,128)(2,1)S(1)}, bf16[128,256]{1,0:T(8,128)(2,1)S(1)}) fusion(f32[8,4,128,256]{3,2,1,0:T(8,128)} %get-tuple-element.58), kind=kLoop, calls=%fused_computation.66 | loop fusion | flops 3080192 | bytes 4325376 | tf_op jit(solution)/shard_map/reduce_sum | solution.py:85
  63.8 0.8 copy.34
  64.6 7.3 %all-to-all-start = ((bf16[16,2,2048]{2,1,0:T(2,128)(2,1)}), bf16[16,2,2048]{2,1,0:T(2,128)(2,1)S(1)}, u32[]{:S(2)}, u32[]{:S(2)}) async-start(bf16[16,2,2048]{2,1,0:T(2,128)(2,1)} %copy.34), calls=%async_computation | async-start | bytes 262144 | tf_op jit(solution)/shard_map/all_to_all | solution.py:24
  71.9 6.1 %all-to-all-done = bf16[16,2,2048]{2,1,0:T(2,128)(2,1)S(1)} async-done(((bf16[16,2,2048]{2,1,0:T(2,128)(2,1)}), bf16[16,2,2048]{2,1,0:T(2,128)(2,1)S(1)}, u32[]{:S(2)}, u32[]{:S(2)}) %all-to-all-start) | async-done | bytes 131104 | tf_op jit(solution)/shard_map/all_to_all | solution.py:24
  78.0 0.1 convert_reduce_fusion
  78.2 0.8 broadcast_in_dim.101
  79.0 9.8 %all-to-all-start.1 = ((f32[16,2,2048]{2,1,0:T(2,128)}), f32[16,2,2048]{2,1,0:T(2,128)S(1)}, u32[]{:S(2)}, u32[]{:S(2)}) async-start(f32[16,2,2048]{2,1,0:T(2,128)} %broadcast_in_dim.101), calls=%async_computation.1 | async-start | bytes 524288 | tf_op jit(solution)/shard_map/all_to_all | solution.py:30
  88.9 4.4 %copy.45 = bf16[4,8,128,256]{3,1,2,0:T(8,128)(2,1)S(1)} copy(f32[4,8,128,256]{3,2,1,0:T(8,128)} %bitcast.64) | data formatting | bytes 6291456
  93.3 6.0 %copy.36 = bf16[32,32768]{0,1:T(8,128)(2,1)} copy(bf16[32,32768]{1,0:T(8,128)(2,1)S(1)} %bitcast.65) | data formatting | bytes 4194304 | tf_op jit(solution)/shard_map/reshape | solution.py:84
  99.3 10.1 %gather_fusion = bf16[2048,32]{1,0:T(8,128)(2,1)S(1)} fusion(bf16[32,32768]{0,1:T(8,128)(2,1)} %copy.36, s32[2048]{0:T(1024)S(1)} %get-tuple-element.82), kind=kCustom, calls=%fused_computation | custom fusion | bytes 270336 | tf_op jit(solution)/shard_map/jit(_take)/gather | solution.py:101
  109.3 0.2 copy.37
  109.6 0.7 select_convert_fusion
  110.3 0.1 reduce_sum.58
  110.3 0.4 copy.38
  110.7 5.5 %gather_fusion.1 = f32[2048,2]{1,0:T(8,128)S(1)} fusion(f32[2,2048]{0,1:T(8,128)S(1)} %copy.38, s32[2048]{0:T(1024)S(1)} %get-tuple-element.83), kind=kCustom, calls=%fused_computation.1 | custom fusion | bytes 40960 | tf_op jit(solution)/shard_map/jit(_take)/gather | solution.py:93
  116.2 0.7 select_bitcast_fusion
  116.9 0.3 copy.39
  117.2 0.8 broadcast_in_dim.111
  118.1 4.3 %all-to-all-start.3 = ((f32[16,2,2048]{2,1,0:T(2,128)}), f32[16,2,2048]{2,1,0:T(2,128)S(1)}, u32[]{:S(2)}, u32[]{:S(2)}) async-start(f32[16,2,2048]{2,1,0:T(2,128)} %broadcast_in_dim.111), calls=%async_computation.3 | async-start | bytes 524288 | tf_op jit(solution)/shard_map/all_to_all | solution.py:30
  122.3 0.6 pad_maximum_fusion
  123.0 6.6 %all-to-all-done.3 = f32[16,2,2048]{2,1,0:T(2,128)S(1)} async-done(((f32[16,2,2048]{2,1,0:T(2,128)}), f32[16,2,2048]{2,1,0:T(2,128)S(1)}, u32[]{:S(2)}, u32[]{:S(2)}) %all-to-all-start.3) | async-done | bytes 262176 | tf_op jit(solution)/shard_map/all_to_all | solution.py:30
  129.6 4.2 %all-to-all-start.2 = ((bf16[32,16,128]{2,0,1:T(8,128)(2,1)}), bf16[32,16,128]{2,0,1:T(8,128)(2,1)S(1)}, u32[]{:S(2)}, u32[]{:S(2)}) async-start(bf16[32,16,128]{2,0,1:T(8,128)(2,1)} %select_convert_fusion), calls=%async_computation.2 | async-start | bytes 262144 | tf_op jit(solution)/shard_map/all_to_all | solution.py:107
  133.8 0.1 reduce_sum.59
  133.9 6.1 %all-to-all-done.2 = bf16[32,16,128]{2,0,1:T(8,128)(2,1)S(1)} async-done(((bf16[32,16,128]{2,0,1:T(8,128)(2,1)}), bf16[32,16,128]{2,0,1:T(8,128)(2,1)S(1)}, u32[]{:S(2)}, u32[]{:S(2)}) %all-to-all-start.2) | async-done | bytes 131104 | tf_op jit(solution)/shard_map/all_to_all | solution.py:107
  140.0 0.7 fusion.30
  (44 shorter events, 1.1 us)
Async XLA Ops:
  61.1 27.8 %copy-start = (s32[2048]{0:T(1024)S(1)}, s32[2048]{0:T(1024)}, u32[]{:S(2)}) copy-start(s32[2048]{0:T(1024)} %param.9) | copy-start | bytes 24580
  64.6 13.4 %all-to-all-start = ((bf16[16,2,2048]{2,1,0:T(2,128)(2,1)}), bf16[16,2,2048]{2,1,0:T(2,128)(2,1)S(1)}, u32[]{:S(2)}, u32[]{:S(2)}) async-start(bf16[16,2,2048]{2,1,0:T(2,128)(2,1)} %copy.34), calls=%async_computation | async-start | bytes 262144 | tf_op jit(solution)/shard_map/all_to_all | solution.py:24
  79.0 31.3 %all-to-all-start.1 = ((f32[16,2,2048]{2,1,0:T(2,128)}), f32[16,2,2048]{2,1,0:T(2,128)S(1)}, u32[]{:S(2)}, u32[]{:S(2)}) async-start(f32[16,2,2048]{2,1,0:T(2,128)} %broadcast_in_dim.101), calls=%async_computation.1 | async-start | bytes 524288 | tf_op jit(solution)/shard_map/all_to_all | solution.py:30
  118.1 11.5 %all-to-all-start.3 = ((f32[16,2,2048]{2,1,0:T(2,128)}), f32[16,2,2048]{2,1,0:T(2,128)S(1)}, u32[]{:S(2)}, u32[]{:S(2)}) async-start(f32[16,2,2048]{2,1,0:T(2,128)} %broadcast_in_dim.111), calls=%async_computation.3 | async-start | bytes 524288 | tf_op jit(solution)/shard_map/all_to_all | solution.py:30
  129.6 10.4 %all-to-all-start.2 = ((bf16[32,16,128]{2,0,1:T(8,128)(2,1)}), bf16[32,16,128]{2,0,1:T(8,128)(2,1)S(1)}, u32[]{:S(2)}, u32[]{:S(2)}) async-start(bf16[32,16,128]{2,0,1:T(8,128)(2,1)} %select_convert_fusion), calls=%async_computation.2 | async-start | bytes 262144 | tf_op jit(solution)/shard_map/all_to_all | solution.py:107
where the time goes:
time: 141 us
  matrix products  55.7 us (40%)
  local copies, waits for them, and re-layouts  29.5 us (21%)
  starting transfers between devices  25.7 us (18%)
  waiting for transfers between devices  18.8 us (13%)
  other arithmetic  9.96 us (7%)
    dot_general x8, matrix products, cell_block(): jnp.einsum('csh,csl->chl', high_table, lower_table, preferred_element_typ...  30.5 us
    dot_general x8, matrix products, cell_block(): jnp.einsum('csh,csl->chl', high_table, upper_table, preferred_element_typ...  25.2 us
    all_to_all x2, starting transfers between devices, copy_for_each(): return lax.all_to_all(copies, axis, split_axis=0, concat_axis=0, tiled=True)  14.1 us
    gather x2, local copies, waits for them, and re-layouts, per_device(): dense = jnp.take(expanded, selected, axis=1)  10.3 us
    all_to_all x1, starting transfers between devices, sum_at_owner(): tiles = lax.all_to_all(split_up(value, dim, length), axis, 0, 0, tiled=True)  7.33 us
    all_to_all x2, waiting for transfers between devices, copy_for_each(): return lax.all_to_all(copies, axis, split_axis=0, concat_axis=0, tiled=True)  6.63 us
    all_to_all x1, waiting for transfers between devices, sum_at_owner(): tiles = lax.all_to_all(split_up(value, dim, length), axis, 0, 0, tiled=True)  6.11 us
    all_to_all x1, waiting for transfers between devices, per_device(): lax.all_to_all(dense.astype(jnp.bfloat16), 'gz', split_axis=1, concat_axi...  6.07 us
  transfers between devices with their start and end apart: 4, of which 3 were waited for; matrix products, arithmetic and copies ran while one was open for 16% of the time, Pallas kernels for 0%

commit v1 on v0

v1 whole, which is shorter than its diff:
```python
import jax
import jax.numpy as jnp
from jax import lax
from jax.experimental import pallas as pl
from jax.experimental.pallas import tpu as pltpu
from jax.sharding import PartitionSpec as P

target_sum = 10000.0
var_floor = 0.01
clip_value = 10.0
MESH = pl.DeviceIdType.MESH
f32, bf16, i32 = jnp.float32, jnp.bfloat16, jnp.int32


def iota(shape, dim):
    return lax.broadcasted_iota(i32, shape, dim)


def vreg_stage(x, j, p):
    n = x.shape[0]
    if p is None:
        y = x.reshape(n >> (j + 1), 2, 1 << j, 8, 128)
        a, b = y[:, 0], y[:, 1]
        out = jnp.stack([jnp.minimum(a, b), jnp.maximum(a, b)], axis=1)
    else:
        y = x.reshape(n >> (p + 1), 2, 1 << (p - j - 1), 2, 1 << j, 8, 128)
        a, b = y[:, :, :, 0], y[:, :, :, 1]
        lo, hi = jnp.minimum(a, b), jnp.maximum(a, b)
        first = jnp.stack([lo[:, 0], hi[:, 1]], axis=1)
        second = jnp.stack([hi[:, 0], lo[:, 1]], axis=1)
        out = jnp.stack([first, second], axis=3)
    return out.reshape(n, 8, 128)


def sublane_stage(x, d):
    rows = iota(x.shape, 1)
    other = jnp.take_along_axis(x, rows ^ d, axis=1, mode="promise_in_bounds")
    return jnp.where((rows & d) == 0, jnp.minimum(x, other), jnp.maximum(x, other))


def lane_stage(x, d):
    flat = x.reshape(x.shape[0] * 8, 128)
    lanes = iota(flat.shape, 1)
    other = jnp.take_along_axis(flat, lanes ^ d, axis=1, mode="promise_in_bounds")
    out = jnp.where((lanes & d) == 0, jnp.minimum(flat, other), jnp.maximum(flat, other))
    return out.reshape(x.shape)


def sort_words(x):
    place = iota((1, 8, 128), 1) * 64 + (iota((1, 8, 128), 2) >> 5) * 512

    def sign(p):
        return jnp.where(((place >> p) & 1) == 0, f32(1.0), f32(-1.0))

    held = None
    for p in range(1, 12):
        if p >= 6:
            change = sign(p) if p < 11 else None
            if held is not None:
                change = held if change is None else change * held
            x = x * change
            held = sign(p)
        for j in reversed(range(p)):
            if j >= 9:
                x = lane_stage(x, 32 << (j - 9))
            elif j >= 6:
                x = sublane_stage(x, 1 << (j - 6))
            else:
                x = vreg_stage(x, j, p if p < 6 else None)
    return x


def make_words(columns, raw):
    place = ((columns << 6) & ((0x600 << 10) | (15 << 6))) | ((columns << 12) & (7 << 16))
    return place | ((columns << 3) & (63 << 10)) | raw


def sort_rows(tiles):
    x = jnp.concatenate(
        [jnp.concatenate(tiles[4 * m : 4 * m + 4], axis=0).T for m in range(4)], axis=0
    )
    x = sort_words(x.reshape(64, 8, 128)).reshape(4, 128, 128)
    turned = [x[m].T for m in range(4)]
    return [turned[owner % 4][32 * (owner // 4) : 32 * (owner // 4) + 32] for owner in range(16)]


def kernel(
    nnz_ref, columns_ref, counts_ref, selected_ref, stats_ref, pca_ref,
    words, packed, scale_ref,
    gene_out, gene_in, pick_out, pick_in, dense_out, dense_in,
    x_out, x_in, xpick_out, xpick_in, y_out, y_in, ypick_out, ypick_in,
    send_gene, recv_gene, send_pick, recv_pick, send_dense, recv_dense,
    send_x, recv_x, send_y, recv_y,
):
    gx, gy, gz = lax.axis_index("gx"), lax.axis_index("gy"), lax.axis_index("gz")
    nx, ny, nz = lax.axis_size("gx"), lax.axis_size("gy"), lax.axis_size("gz")
    cells = 32 * nx * ny * nz

    barrier = pltpu.get_barrier_semaphore()

    def greet(axis, me, n):
        def one(d, carry):
            pl.semaphore_signal(
                barrier, inc=1, device_id={axis: lax.rem(me + d, n)}, device_id_type=MESH
            )
            return carry

        lax.fori_loop(1, n, one, 0)

    greet("gz", gz, nz)
    greet("gx", gx, nx)
    greet("gy", gy, ny)

    rows = iota((32, 1), 0)
    live = jnp.zeros((32, 1), i32)
    for c in range(32):
        live = jnp.where(rows == c, nnz_ref[c], live)
    tiles, library = [], jnp.zeros((32, 128), f32)
    for t in range(16):
        part = pl.ds(128 * t, 128)
        slot = iota((32, 128), 1) + 128 * t
        raw = jnp.where(slot < live, counts_ref[:, part], 0)
        library = library + raw.astype(f32)
        tiles.append(make_words(columns_ref[:, part], raw).astype(f32))
    scale = target_sum / jnp.sum(library, axis=1, keepdims=True)
    scale_ref[...] = jnp.broadcast_to(scale, (32, 128))
    for owner, tile in enumerate(sort_rows(tiles)):
        word = tile.astype(i32) & 1023
        words[owner] = word
        packed[owner] = (word[:16] << 10) | word[16:]

    pick = (iota((16, 256), 1) >> 4) == iota((16, 256), 0)
    pick = jnp.where(pick, f32(1.0), f32(0.0)).astype(bf16)

    def gene_sums(t, carry):
        word = words[t]
        value = jnp.log(1.0 + (word & 63).astype(f32) * scale_ref[...])
        low = (word >> 6).astype(f32).astype(bf16)
        terms = []
        for term in (value.astype(bf16), (value * value).astype(bf16)):
            folded = []
            for l in range(16):
                kept = jnp.where(low == bf16(l), term, bf16(0.0))
                folded.append(kept[:16] + kept[16:])
            terms.append(jnp.concatenate(folded, axis=0))
        terms = jnp.concatenate(terms, axis=1)
        sums = jnp.dot(pick, terms, preferred_element_type=f32)
        gene_out[t] = sums.astype(bf16)
        return carry

    lax.fori_loop(0, nz, gene_sums, 0)

    pl.semaphore_wait(barrier, (nx - 1) + (ny - 1) + (nz - 1))

    def to(axis, me, n, d, out, into, send, recv, whole=False):
        other = lax.rem(me + d, n)
        return pltpu.make_async_remote_copy(
            src_ref=out if whole else out.at[other],
            dst_ref=into.at[me],
            send_sem=send.at[other],
            recv_sem=recv.at[me],
            device_id={axis: other},
            device_id_type=MESH,
        )

    def came(axis, me, n, d, out, into, send, recv, whole=False):
        other = lax.rem(me + d, n)
        return pltpu.make_async_remote_copy(
            src_ref=out if whole else out.at[other],
            dst_ref=into.at[other],
            send_sem=send.at[other],
            recv_sem=recv.at[other],
            device_id={axis: other},
            device_id_type=MESH,
        )

    def start(*args, **kw):
        n = args[2]

        def one(d, carry):
            to(*args[:3], d, *args[3:], **kw).start()
            return carry

        lax.fori_loop(1, n, one, 0)

    def finish(*args, **kw):
        n = args[2]

        def one(d, carry):
            copy = came(*args[:3], d, *args[3:], **kw)
            copy.wait_recv()
            copy.wait_send()
            return carry

        lax.fori_loop(1, n, one, 0)

    z = ("gz", gz, nz)
    gene = z + (gene_out, gene_in, send_gene, recv_gene)
    picks = z + (pick_out, pick_in, send_pick, recv_pick)
    dense = z + (dense_out, dense_in, send_dense, recv_dense)
    start(*gene)

    def gather(k, carry):
        gene_id = selected_ref[pl.ds(k, 1), :]
        block = gene_id >> 4
        lane = jnp.broadcast_to(block & 127, (16, 128))
        tile = block >> 7
        got = jnp.zeros((16, 128), i32)
        for t in range(16):
            here = jnp.take_along_axis(packed[t], lane, axis=1, mode="promise_in_bounds")
            got = jnp.where(tile == t, here, got)
        word = jnp.concatenate([got >> 10, got & 1023], axis=0)
        count = jnp.where((word >> 6) == (gene_id & 15), word & 63, 0).astype(f32)
        value = jnp.log(1.0 + count * scale_ref[...])
        dense_out[k] = value.astype(bf16)
        pick_out[k] = jnp.concatenate(
            [jnp.sum(value, axis=0, keepdims=True), jnp.sum(value * value, axis=0, keepdims=True)],
            axis=0,
        )
        return carry

    lax.fori_loop(0, nz, gather, 0)
    start(*picks)
    start(*dense)
    gene_in[gz] = gene_out[gz]
    pick_in[gz] = pick_out[gz]
    dense_in[gz] = dense_out[gz]

    finish(*gene)
    finish(*picks)
    x_out[...] = jnp.sum(gene_in[...].astype(f32), axis=0)
    xpick_out[...] = jnp.sum(pick_in[...], axis=0)

    def add_over(axis, me, n, out, into, pick_out_, pick_in_, send, recv):
        a = (axis, me, n, out, into, send.at[0], recv.at[0])
        b = (axis, me, n, pick_out_, pick_in_, send.at[1], recv.at[1])
        start(*a, whole=True)
        start(*b, whole=True)
        into[me] = out[...]
        pick_in_[me] = pick_out_[...]
        finish(*a, whole=True)
        finish(*b, whole=True)
        return jnp.sum(into[...], axis=0), jnp.sum(pick_in_[...], axis=0)

    y_out[...], ypick_out[...] = add_over(
        "gx", gx, nx, x_out, x_in, xpick_out, xpick_in, send_x, recv_x
    )
    sums, picked = add_over("gy", gy, ny, y_out, y_in, ypick_out, ypick_in, send_y, recv_y)

    mean = sums[:, :128] / cells
    stats_ref[0] = mean
    stats_ref[1] = sums[:, 128:] / cells - mean * mean

    sel_mean = picked[0:1] / cells
    sel_variance = picked[1:2] / cells - sel_mean * sel_mean
    factor = 1.0 / jnp.sqrt(jnp.maximum(sel_variance, var_floor))
    finish(*dense)
    for s in range(16):
        value = (dense_in[s].astype(f32) - sel_mean) * factor
        pca_ref[32 * s : 32 * s + 32] = jnp.clip(value, -clip_value, clip_value).astype(bf16)


def per_device(columns, counts, nnz_count, selected):
    nz = lax.axis_size("gz")
    vmem = pl.BlockSpec(memory_space=pltpu.VMEM)
    dma = pltpu.SemaphoreType.DMA
    stats, pca = pl.pallas_call(
        kernel,
        out_shape=(
            jax.ShapeDtypeStruct((2, 16, 128), f32),
            jax.ShapeDtypeStruct((512, 128), bf16),
        ),
        in_specs=[pl.BlockSpec(memory_space=pltpu.SMEM), vmem, vmem, vmem],
        out_specs=(vmem, vmem),
        scratch_shapes=[
            pltpu.VMEM((16, 32, 128), i32),
            pltpu.VMEM((16, 16, 128), i32),
            pltpu.VMEM((32, 128), f32),
            pltpu.VMEM((16, 16, 256), bf16),
            pltpu.VMEM((16, 16, 256), bf16),
            pltpu.VMEM((16, 2, 128), f32),
            pltpu.VMEM((16, 2, 128), f32),
            pltpu.VMEM((16, 32, 128), bf16),
            pltpu.VMEM((16, 32, 128), bf16),
            pltpu.VMEM((16, 256), f32),
            pltpu.VMEM((4, 16, 256), f32),
            pltpu.VMEM((2, 128), f32),
            pltpu.VMEM((4, 2, 128), f32),
            pltpu.VMEM((16, 256), f32),
            pltpu.VMEM((4, 16, 256), f32),
            pltpu.VMEM((2, 128), f32),
            pltpu.VMEM((4, 2, 128), f32),
            dma((16,)), dma((16,)), dma((16,)), dma((16,)), dma((16,)), dma((16,)),
            dma((2, 4)), dma((2, 4)), dma((2, 4)), dma((2, 4)),
        ],
        compiler_params=pltpu.CompilerParams(collective_id=0, has_side_effects=True),
    )(nnz_count, columns, counts, selected.reshape(16, 128))
    return stats.transpose(0, 2, 1).reshape(2, 2048), pca


def solution(mesh):
    return jax.shard_map(
        per_device,
        mesh=mesh,
        in_specs=(
            P(("gx", "gy", "gz"), None),
            P(("gx", "gy", "gz"), None),
            P(("gx", "gy", "gz")),
            P(),
        ),
        out_specs=(P(None, "gz"), P(("gx", "gy"), "gz")),
        check_vma=False,
    )
```

time: 141 us -> 31.8 us (0.23)
  matrix products: 55.7 us -> 0 us
  Pallas kernels: 0 us -> 28.8 us
  local copies, waits for them, and re-layouts: 29.5 us -> 2.23 us
  starting transfers between devices: 25.7 us -> 0 us
  waiting for transfers between devices: 18.8 us -> 0 us
  other arithmetic: 9.96 us -> 0 us
    dot_general x16 -> x0, matrix products: 55.7 us -> none  [the longest x8 30.5 us: cell_block(): jnp.einsum('csh,csl->chl', high_table, lower_table, preferred_element_typ...]
    pallas_call x0 -> x1, Pallas kernels: none -> 28.8 us  [per_device(): pl.pallas_call(kernel, out_shape=(jax.ShapeDtypeStruct((2, 16, 128), f32)...]
    all_to_all x4 -> x0, starting transfers between devices: 25.7 us -> none  [the longest x2 14.1 us: copy_for_each(): return lax.all_to_all(copies, axis, split_axis=0, concat_axis=0, tiled=True)]
    all_to_all x4 -> x0, waiting for transfers between devices: 18.8 us -> none  [the longest x2 6.63 us: copy_for_each(): return lax.all_to_all(copies, axis, split_axis=0, concat_axis=0, tiled=True)]
    gather x3 -> x0, local copies, waits for them, and re-layouts: 15.7 us -> none  [the longest x2 10.3 us: per_device(): dense = jnp.take(expanded, selected, axis=1)]
    reshape x3 -> x1, local copies, waits for them, and re-layouts: 6.14 us -> 0.72 us  [per_device(): return (stats.transpose(0, 2, 1).reshape(2, 2048), pca)]
    reduce_sum x5 -> x0, other arithmetic: 4.08 us -> none  [the longest x1 2.62 us: per_device(): total = jnp.sum(expanded, axis=0)]
    unnamed x3, local copies, waits for them, and re-layouts: 4.42 us -> 0.66 us
  transfers between devices with their start and end apart: 4 -> 0, of which waited for: 3 -> 0; matrix products, arithmetic and copies ran while one was open for 16% -> 0% of each run, Pallas kernels for 0% -> 0%
where the time goes in v1:
time: 31.8 us; the launch traced here: 31.7 us
  Pallas kernels  28.8 us (91%)
  local copies, waits for them, and re-layouts  2.23 us (7%)
  between operations  0.65 us (2%)
    pallas_call x1, Pallas kernels, per_device(): pl.pallas_call(kernel, out_shape=(jax.ShapeDtypeStruct((2, 16, 128), f32)...  28.8 us
    transpose x1, local copies, waits for them, and re-layouts, per_device(): return (stats.transpose(0, 2, 1).reshape(2, 2048), pca)  0.85 us
    reshape x1, local copies, waits for them, and re-layouts, per_device(): return (stats.transpose(0, 2, 1).reshape(2, 2048), pca)  0.72 us
    unnamed x3, local copies, waits for them, and re-layouts  0.66 us

profile of v1, /device:TPU:1, one launch (start us, length us, event | category | flops | bytes accessed | tf_op | source)
XLA Modules:
  0.0 31.7 jit_solution(10197878594115625468)
XLA Ops:
  0.6 28.8 %shard_map.59 = (f32[2,16,128]{2,1,0:T(8,128)}, bf16[512,128]{1,0:T(8,128)(2,1)}) custom-call(s32[32]{0:T(128)} %nnz_ref.1, s32[32,2048]{1,0:T(8,128)} %columns_ref.1, s32[32,2048]{1,0:T(8,128)} %counts_ref.1, s32[16,128]{1,0:T(8,128)} %bitcast.3), custom_call_target="tpu_custom_call" | custom-call | tf_op jit(solution)/shard_map/pallas_call | solution.py:267
  29.5 0.0 copy-start
  29.5 0.9 %copy.6 = f32[2,128,16]{2,1,0:T(8,128)S(1)} copy(f32[2,128,16]{1,2,0:T(8,128)} %bitcast.2) | data formatting | bytes 32768 | tf_op jit(solution)/shard_map/transpose | solution.py:298
  30.3 0.7 %reshape.11 = f32[2,2048]{1,0:T(2,128)} reshape(f32[2,128,16]{2,1,0:T(8,128)S(1)} %copy.6) | data formatting | bytes 32768 | tf_op jit(solution)/shard_map/reshape | solution.py:298
  31.1 0.0 copy-done
  31.1 0.7 %copy.8 = bf16[512,128]{1,0:T(8,128)(2,1)} copy(bf16[512,128]{1,0:T(8,128)(2,1)S(1)} %copy-done) | data formatting | bytes 262144
Async XLA Ops:
  29.5 1.6 %copy-start = (bf16[512,128]{1,0:T(8,128)(2,1)S(1)}, bf16[512,128]{1,0:T(8,128)(2,1)}, u32[]{:S(2)}) copy-start(bf16[512,128]{1,0:T(8,128)(2,1)} %get-tuple-element.9) | copy-start | bytes 393220

commit v2 on v1

--- a/solution.py
+++ b/solution.py
@@ -82,6 +82,14 @@
     x = sort_words(x.reshape(64, 8, 128)).reshape(4, 128, 128)
     turned = [x[m].T for m in range(4)]
     return [turned[owner % 4][32 * (owner // 4) : 32 * (owner // 4) + 32] for owner in range(16)]
+
+
+def in_gene_order(stat):
+    lanes = (iota((16, 128), 1) & 15) * 8
+    parts = [
+        jnp.take_along_axis(stat, lanes + r, axis=1, mode="promise_in_bounds") for r in range(8)
+    ]
+    return jnp.concatenate(parts, axis=0).T[:16]
 
 
 def kernel(
@@ -132,7 +140,7 @@
     pick = (iota((16, 256), 1) >> 4) == iota((16, 256), 0)
     pick = jnp.where(pick, f32(1.0), f32(0.0)).astype(bf16)
 
-    def gene_sums(t, carry):
+    def gene_sums(t):
         word = words[t]
         value = jnp.log(1.0 + (word & 63).astype(f32) * scale_ref[...])
         low = (word >> 6).astype(f32).astype(bf16)
@@ -146,9 +154,9 @@
         terms = jnp.concatenate(terms, axis=1)
         sums = jnp.dot(pick, terms, preferred_element_type=f32)
         gene_out[t] = sums.astype(bf16)
-        return carry
-
-    lax.fori_loop(0, nz, gene_sums, 0)
+
+    for t in range(16):
+        gene_sums(t)
 
     pl.semaphore_wait(barrier, (nx - 1) + (ny - 1) + (nz - 1))
 
@@ -200,8 +208,8 @@
     dense = z + (dense_out, dense_in, send_dense, recv_dense)
     start(*gene)
 
-    def gather(k, carry):
-        gene_id = selected_ref[pl.ds(k, 1), :]
+    def gather(k):
+        gene_id = selected_ref[k : k + 1, :]
         block = gene_id >> 4
         lane = jnp.broadcast_to(block & 127, (16, 128))
         tile = block >> 7
@@ -217,9 +225,9 @@
             [jnp.sum(value, axis=0, keepdims=True), jnp.sum(value * value, axis=0, keepdims=True)],
             axis=0,
         )
-        return carry
-
-    lax.fori_loop(0, nz, gather, 0)
+
+    for k in range(16):
+        gather(k)
     start(*picks)
     start(*dense)
     gene_in[gz] = gene_out[gz]
@@ -248,8 +256,11 @@
     sums, picked = add_over("gy", gy, ny, y_out, y_in, ypick_out, ypick_in, send_y, recv_y)
 
     mean = sums[:, :128] / cells
-    stats_ref[0] = mean
-    stats_ref[1] = sums[:, 128:] / cells - mean * mean
+    variance = sums[:, 128:] / cells - mean * mean
+    for row, stat in enumerate((mean, variance)):
+        flat = in_gene_order(stat)
+        for u in range(16):
+            stats_ref[row : row + 1, 128 * u : 128 * u + 128] = flat[u : u + 1]
 
     sel_mean = picked[0:1] / cells
     sel_variance = picked[1:2] / cells - sel_mean * sel_mean
@@ -267,8 +278,8 @@
     stats, pca = pl.pallas_call(
         kernel,
         out_shape=(
-            jax.ShapeDtypeStruct((2, 16, 128), f32),
-            jax.ShapeDtypeStruct((512, 128), bf16),
+            pltpu.VMEM((2, 2048), f32),
+            pltpu.VMEM((512, 128), bf16),
         ),
         in_specs=[pl.BlockSpec(memory_space=pltpu.SMEM), vmem, vmem, vmem],
         out_specs=(vmem, vmem),
@@ -295,7 +306,7 @@
         ],
         compiler_params=pltpu.CompilerParams(collective_id=0, has_side_effects=True),
     )(nnz_count, columns, counts, selected.reshape(16, 128))
-    return stats.transpose(0, 2, 1).reshape(2, 2048), pca
+    return stats, pca
 
 
 def solution(mesh):

time: 31.8 us -> 27.2 us (0.86)
  Pallas kernels: 28.8 us -> 25.2 us
  local copies, waits for them, and re-layouts: 2.23 us -> 1.26 us
    pallas_call x1, Pallas kernels: 28.8 us -> 25.2 us  [per_device(): pl.pallas_call(kernel, out_shape=(pltpu.VMEM((2, 2048), f32), pltpu.VMEM(...]
    transpose x1 -> x0, local copies, waits for them, and re-layouts: 0.85 us -> none  [per_device(): return (stats.transpose(0, 2, 1).reshape(2, 2048), pca)]
    reshape x1 -> x0, local copies, waits for them, and re-layouts: 0.72 us -> none  [per_device(): return (stats.transpose(0, 2, 1).reshape(2, 2048), pca)]
    unnamed x3 -> x2, local copies, waits for them, and re-layouts: 0.66 us -> 1.26 us
where the time goes in v2:
time: 27.2 us; the launch traced here: 27.1 us
  Pallas kernels  25.2 us (93%)
  local copies, waits for them, and re-layouts  1.26 us (5%)
  between operations  0.64 us (2%)
    pallas_call x1, Pallas kernels, per_device(): pl.pallas_call(kernel, out_shape=(pltpu.VMEM((2, 2048), f32), pltpu.VMEM(...  25.2 us
    unnamed x2, local copies, waits for them, and re-layouts  1.26 us

profile of v2, /device:TPU:1, one launch (start us, length us, event | category | flops | bytes accessed | tf_op | source)
XLA Modules:
  0.0 27.1 jit_solution(8765384305695789159)
XLA Ops:
  0.6 25.2 %shard_map.59 = (f32[2,2048]{1,0:T(2,128)S(1)}, bf16[512,128]{1,0:T(8,128)(2,1)S(1)}) custom-call(s32[32]{0:T(128)} %nnz_ref.1, s32[32,2048]{1,0:T(8,128)} %columns_ref.1, s32[32,2048]{1,0:T(8,128)} %counts_ref.1, s32[16,128]{1,0:T(8,128)} %bitcast.1), custom_call_target="tpu_custom_call" | custom-call | tf_op jit(solution)/shard_map/pallas_call | solution.py:278
  25.8 0.6 %copy.8 = f32[2,2048]{1,0:T(2,128)} copy(f32[2,2048]{1,0:T(2,128)S(1)} %get-tuple-element.2) | data formatting | bytes 32768
  26.4 0.7 %copy.9 = bf16[512,128]{1,0:T(8,128)(2,1)} copy(bf16[512,128]{1,0:T(8,128)(2,1)S(1)} %get-tuple-element.3) | data formatting | bytes 262144
